TPU v7x, 32 devices: a whole 2x2x4 slice. The times are simulated.
32 devices in a mesh: slab: 16 (over z, y, x), energy: 2 (over core).
Axes of the slice: x: 2, y: 2, z: 4, core: 2. Of those that a mesh axis runs over, the one named last changes fastest.
Arguments:
- onsite_energy: float32 [32, 128], P('slab'), may hold values from -0.3 to 0.3
- onsite_mixing: float32 [32, 128, 128], P('slab'), may hold values from -0.15625 to 0.15625
- hop_strength: float32 [32, 128], P('slab'), may hold values from 0.8 to 1.2
- hop_mixing: float32 [32, 128, 128], P('slab'), may hold values from -0.15625 to 0.15625
- energy: float32 [2], P('energy'), parts along dimension 0, may hold values from -0.4 to 0.4
- broadening: float32 [2], P('energy'), parts along dimension 0, may hold values from 0.01 to 0.025
Outputs:
- green_real: float32 [64, 128, 128], P(('energy', 'slab')), parts along dimension 0
- green_imag: float32 [64, 128, 128], P(('energy', 'slab')), parts along dimension 0
There are 2 independent parts, one for each index of `energy`. A program takes and returns all parts, laid end to end along the dimension named above; an argument that names none is the same for every part. Nothing has to cross between parts.
All inputs are finite; a program needn't handle non-finite values.
Results may differ from a plain program's by a relative error of at most 0.0007.
Values sent between devices are 32-bit elements; how exact they have to be, the bound alone decides.
A program may use at most 128 MiB of HBM per device.

v0:
```python
import jax
import jax.numpy as jnp
from jax import lax
from jax.sharding import PartitionSpec as P


def passed_along(block, axis, distance):
    devices = range(lax.axis_size(axis))
    route = [(i - distance, i) for i in devices if i - distance in devices]
    return lax.ppermute(block, axis, route)


def real_product(first, second):
    return jnp.dot(
        first, second, precision=lax.Precision.HIGHEST, preferred_element_type=jnp.float32
    )


def complex_product(first, second):
    return (
        real_product(first[0], second[0]) - real_product(first[1], second[1]),
        real_product(first[0], second[1]) + real_product(first[1], second[0]),
    )


def transposed(block):
    return (block[0].T, block[1].T)


def negated(block):
    return (-block[0], -block[1])


def combined(first, second, factor):
    return (first[0] + factor * second[0], first[1] + factor * second[1])


def unpack(values, offset):
    return ((values[offset], values[offset + 1]), (values[offset + 2], values[offset + 3]))


def invert_single(real_part, imag_part):
    block = (real_part, imag_part)
    orbitals = real_part.shape[0]
    adjoint = (real_part.T, -imag_part.T)
    normal = complex_product(adjoint, block)
    stacked = jnp.concatenate(
        [
            jnp.concatenate([normal[0], -normal[1]], axis=1),
            jnp.concatenate([normal[1], normal[0]], axis=1),
        ],
        axis=0,
    )
    factor = jnp.linalg.cholesky(stacked)
    solved = jax.scipy.linalg.cho_solve(
        (factor, True), jnp.concatenate([adjoint[0], adjoint[1]], axis=0)
    )
    estimate = (solved[:orbitals], solved[orbitals:])
    identity = jnp.eye(orbitals, dtype=jnp.float32)
    for refinement in range(2):
        residue = complex_product(block, estimate)
        estimate = complex_product(estimate, (2.0 * identity - residue[0], -residue[1]))
    return estimate


def invert_pair(first_block, second_block):
    real_parts = jnp.stack([first_block[0], second_block[0]], axis=0)
    imag_parts = jnp.stack([first_block[1], second_block[1]], axis=0)
    inverse_real, inverse_imag = jax.vmap(invert_single)(real_parts, imag_parts)
    return ((inverse_real[0], inverse_imag[0]), (inverse_real[1], inverse_imag[1]))


def outgoing(state, inverse):
    block, low_link, high_link = state
    weight_low = complex_product(inverse, low_link)
    weight_high = complex_product(inverse, high_link)
    upward = (
        complex_product(transposed(high_link), weight_high),
        negated(complex_product(transposed(high_link), weight_low)),
    )
    downward = (
        complex_product(transposed(low_link), weight_low),
        negated(complex_product(transposed(low_link), weight_high)),
    )
    return (upward, downward)


def outgoing_both(first_state, second_state):
    first_inverse, second_inverse = invert_pair(first_state[0], second_state[0])
    return (outgoing(first_state, first_inverse), outgoing(second_state, second_inverse))


def absorb(state, from_lower, from_upper):
    block, low_link, high_link = state
    block = combined(combined(block, from_lower[0], -1.0), from_upper[0], -1.0)
    return (block, from_lower[1], from_upper[1])


def shards(onsite_energy, onsite_mixing, hop_strength, hop_mixing, energy, broadening):
    orbitals = onsite_mixing.shape[1]
    slab_count = lax.axis_size("slab")
    level_count = slab_count.bit_length() - 1
    position = lax.axis_index("slab")
    identity = jnp.eye(orbitals, dtype=jnp.float32)
    zero_block = jnp.zeros((orbitals, orbitals), jnp.float32)

    def onsite_block(index):
        mixing = onsite_mixing[index]
        hamilton = jnp.diag(onsite_energy[index]) + 0.5 * (mixing + mixing.T)
        return (energy[0] * identity - hamilton, broadening[0] * identity)

    first_link = -(jnp.diag(hop_strength[0]) + hop_mixing[0])
    second_link = jnp.where(
        position < slab_count - 1, -(jnp.diag(hop_strength[1]) + hop_mixing[1]), 0.0
    )
    arrived = passed_along(second_link, "slab", 1)
    first_state = (onsite_block(0), (arrived.T, zero_block), (first_link, zero_block))
    second_state = (onsite_block(1), (first_link.T, zero_block), (second_link, zero_block))
    (first_up, first_down), (second_up, second_down) = outgoing_both(first_state, second_state)
    from_below = passed_along(
        (second_up[0][0], second_up[0][1], second_up[1][0], second_up[1][1]), "slab", 1
    )
    from_above = passed_along(
        (first_down[0][0], first_down[0][1], first_down[1][0], first_down[1][1]), "slab", -1
    )
    first_state, second_state = (
        absorb(first_state, unpack(from_below, 0), second_down),
        absorb(second_state, first_up, unpack(from_above, 0)),
    )
    for level_index in range(level_count):
        stride = 1 << level_index
        (first_up, first_down), (second_up, second_down) = outgoing_both(first_state, second_state)
        rising = passed_along(
            (
                first_up[0][0],
                first_up[0][1],
                first_up[1][0],
                first_up[1][1],
                second_up[0][0],
                second_up[0][1],
                second_up[1][0],
                second_up[1][1],
            ),
            "slab",
            stride,
        )
        falling = passed_along(
            (
                first_down[0][0],
                first_down[0][1],
                first_down[1][0],
                first_down[1][1],
                second_down[0][0],
                second_down[0][1],
                second_down[1][0],
                second_down[1][1],
            ),
            "slab",
            -stride,
        )
        first_state, second_state = (
            absorb(first_state, unpack(rising, 0), unpack(falling, 0)),
            absorb(second_state, unpack(rising, 4), unpack(falling, 4)),
        )
    first_green, second_green = invert_pair(first_state[0], second_state[0])
    return (
        jnp.stack([first_green[0], second_green[0]], axis=0),
        jnp.stack([first_green[1], second_green[1]], axis=0),
    )


def solution(mesh):
    return jax.shard_map(
        shards,
        mesh=mesh,
        in_specs=(
            P("slab", None),
            P("slab", None, None),
            P("slab", None),
            P("slab", None, None),
            P("energy"),
            P("energy"),
        ),
        out_specs=(P(("energy", "slab"), None, None), P(("energy", "slab"), None, None)),
        check_vma=False,
    )
```

profile of v0, /device:TPU:0, one launch (start us, length us, event | category | flops | bytes accessed | tf_op | source)
XLA Modules:
  0.0 1009.1 jit_solution(13311264582571112456)
XLA Ops:
  2.2 5.0 collective-permute-start.1
  11.4 23.5 %custom-call.35 = f32[2,128,128]{2,1,0:T(8,128)S(1)} custom-call(f32[2,128,128]{2,1,0:T(8,128)S(1)} %cholesky.502), custom_call_target="Cholesky" | custom-call | tf_op jit(solution)/shard_map/vmap(jit(cholesky))/cholesky | solution.py:54
  34.9 19.7 %custom-call.36 = f32[2,1,128,128]{2,3,1,0:T(8,128)S(1)} custom-call(f32[2,1,128,128]{3,2,1,0:T(8,128)S(1)} %select_bitcast_fusion.5), custom_call_target="InvertDiagBlocksLowerTriangular" | custom-call | tf_op jit(solution)/shard_map/vmap(jit(cholesky))/cholesky | solution.py:54
  55.3 23.5 %custom-call.37 = f32[2,128,128]{2,1,0:T(8,128)S(1)} custom-call(f32[2,128,128]{2,1,0:T(8,128)S(1)} %convolution_subtract_fusion.46), custom_call_target="Cholesky" | custom-call | tf_op jit(solution)/shard_map/vmap(jit(cholesky))/cholesky | solution.py:54
  83.5 39.5 %custom-call.38 = f32[2,2,128,128]{2,3,1,0:T(8,128)S(1)} custom-call(f32[2,2,128,128]{3,2,1,0:T(8,128)S(1)} %bitcast.1069), custom_call_target="InvertDiagBlocksLowerTriangular" | custom-call | tf_op jit(solution)/shard_map/vmap(jit(_cho_solve))/triangular_solve | solution.py:55
  163.1 23.5 %custom-call.39 = f32[2,128,128]{2,1,0:T(8,128)S(1)} custom-call(f32[2,128,128]{2,1,0:T(8,128)S(1)} %cholesky.505), custom_call_target="Cholesky" | custom-call | tf_op jit(solution)/shard_map/vmap(jit(cholesky))/cholesky | solution.py:54
  186.6 19.7 %custom-call.40 = f32[2,1,128,128]{2,3,1,0:T(8,128)S(1)} custom-call(f32[2,1,128,128]{3,2,1,0:T(8,128)S(1)} %select_bitcast_fusion.4), custom_call_target="InvertDiagBlocksLowerTriangular" | custom-call | tf_op jit(solution)/shard_map/vmap(jit(cholesky))/cholesky | solution.py:54
  207.0 23.5 %custom-call.41 = f32[2,128,128]{2,1,0:T(8,128)S(1)} custom-call(f32[2,128,128]{2,1,0:T(8,128)S(1)} %convolution_subtract_fusion.38), custom_call_target="Cholesky" | custom-call | tf_op jit(solution)/shard_map/vmap(jit(cholesky))/cholesky | solution.py:54
  235.0 39.5 %custom-call.42 = f32[2,2,128,128]{2,3,1,0:T(8,128)S(1)} custom-call(f32[2,2,128,128]{3,2,1,0:T(8,128)S(1)} %bitcast.1070), custom_call_target="InvertDiagBlocksLowerTriangular" | custom-call | tf_op jit(solution)/shard_map/vmap(jit(_cho_solve))/triangular_solve | solution.py:55
  285.6 6.3 collective-permute-start.14
  297.7 5.9 collective-permute-start.16
  310.4 5.5 collective-permute-start.5
  317.8 4.9 collective-permute-start.12
  325.9 4.8 collective-permute-done.13
  330.7 4.8 collective-permute-start.21
  336.0 5.2 collective-permute-start.20
  344.1 23.5 %custom-call.43 = f32[2,128,128]{2,1,0:T(8,128)S(1)} custom-call(f32[2,128,128]{2,1,0:T(8,128)S(1)} %cholesky.508), custom_call_target="Cholesky" | custom-call | tf_op jit(solution)/shard_map/vmap(jit(cholesky))/cholesky | solution.py:54
  367.6 19.7 %custom-call.44 = f32[2,1,128,128]{2,3,1,0:T(8,128)S(1)} custom-call(f32[2,1,128,128]{3,2,1,0:T(8,128)S(1)} %select_bitcast_fusion.3), custom_call_target="InvertDiagBlocksLowerTriangular" | custom-call | tf_op jit(solution)/shard_map/vmap(jit(cholesky))/cholesky | solution.py:54
  387.9 23.5 %custom-call.45 = f32[2,128,128]{2,1,0:T(8,128)S(1)} custom-call(f32[2,128,128]{2,1,0:T(8,128)S(1)} %convolution_subtract_fusion.30), custom_call_target="Cholesky" | custom-call | tf_op jit(solution)/shard_map/vmap(jit(cholesky))/cholesky | solution.py:54
  416.0 39.5 %custom-call.46 = f32[2,2,128,128]{2,3,1,0:T(8,128)S(1)} custom-call(f32[2,2,128,128]{3,2,1,0:T(8,128)S(1)} %bitcast.1071), custom_call_target="InvertDiagBlocksLowerTriangular" | custom-call | tf_op jit(solution)/shard_map/vmap(jit(_cho_solve))/triangular_solve | solution.py:55
  464.4 7.0 collective-permute-start.28
  472.1 4.8 collective-permute-start.27
  488.1 5.0 collective-permute-start.32
  503.4 5.5 collective-permute-start.19
  510.8 4.9 collective-permute-start.26
  523.1 4.8 collective-permute-start.37
  535.2 23.5 %custom-call.47 = f32[2,128,128]{2,1,0:T(8,128)S(1)} custom-call(f32[2,128,128]{2,1,0:T(8,128)S(1)} %cholesky.511), custom_call_target="Cholesky" | custom-call | tf_op jit(solution)/shard_map/vmap(jit(cholesky))/cholesky | solution.py:54
  558.7 19.7 %custom-call.48 = f32[2,1,128,128]{2,3,1,0:T(8,128)S(1)} custom-call(f32[2,1,128,128]{3,2,1,0:T(8,128)S(1)} %select_bitcast_fusion.2), custom_call_target="InvertDiagBlocksLowerTriangular" | custom-call | tf_op jit(solution)/shard_map/vmap(jit(cholesky))/cholesky | solution.py:54
  579.0 23.5 %custom-call.49 = f32[2,128,128]{2,1,0:T(8,128)S(1)} custom-call(f32[2,128,128]{2,1,0:T(8,128)S(1)} %convolution_subtract_fusion.22), custom_call_target="Cholesky" | custom-call | tf_op jit(solution)/shard_map/vmap(jit(cholesky))/cholesky | solution.py:54
  607.3 39.5 %custom-call.50 = f32[2,2,128,128]{2,3,1,0:T(8,128)S(1)} custom-call(f32[2,2,128,128]{3,2,1,0:T(8,128)S(1)} %bitcast.1072), custom_call_target="InvertDiagBlocksLowerTriangular" | custom-call | tf_op jit(solution)/shard_map/vmap(jit(_cho_solve))/triangular_solve | solution.py:55
  655.7 5.4 collective-permute-start.43
  661.8 4.8 collective-permute-start.44
  670.6 4.6 collective-permute-start.46
  677.9 4.6 collective-permute-start.48
  692.7 4.6 collective-permute-start.35
  719.1 23.5 %custom-call.51 = f32[2,128,128]{2,1,0:T(8,128)S(1)} custom-call(f32[2,128,128]{2,1,0:T(8,128)S(1)} %cholesky.514), custom_call_target="Cholesky" | custom-call | tf_op jit(solution)/shard_map/vmap(jit(cholesky))/cholesky | solution.py:54
  742.6 19.7 %custom-call.52 = f32[2,1,128,128]{2,3,1,0:T(8,128)S(1)} custom-call(f32[2,1,128,128]{3,2,1,0:T(8,128)S(1)} %select_bitcast_fusion.1), custom_call_target="InvertDiagBlocksLowerTriangular" | custom-call | tf_op jit(solution)/shard_map/vmap(jit(cholesky))/cholesky | solution.py:54
  763.0 23.5 %custom-call.53 = f32[2,128,128]{2,1,0:T(8,128)S(1)} custom-call(f32[2,128,128]{2,1,0:T(8,128)S(1)} %convolution_subtract_fusion.14), custom_call_target="Cholesky" | custom-call | tf_op jit(solution)/shard_map/vmap(jit(cholesky))/cholesky | solution.py:54
  790.8 39.5 %custom-call.54 = f32[2,2,128,128]{2,3,1,0:T(8,128)S(1)} custom-call(f32[2,2,128,128]{3,2,1,0:T(8,128)S(1)} %bitcast.1073), custom_call_target="InvertDiagBlocksLowerTriangular" | custom-call | tf_op jit(solution)/shard_map/vmap(jit(_cho_solve))/triangular_solve | solution.py:55
  839.2 5.2 collective-permute-start.59
  856.4 5.4 collective-permute-start.63
  865.2 5.7 collective-permute-start.51
  874.0 5.4 collective-permute-start.57
  881.3 5.3 collective-permute-done.60
  888.6 23.5 %custom-call.55 = f32[2,128,128]{2,1,0:T(8,128)S(1)} custom-call(f32[2,128,128]{2,1,0:T(8,128)S(1)} %cholesky.517), custom_call_target="Cholesky" | custom-call | tf_op jit(solution)/shard_map/vmap(jit(cholesky))/cholesky | solution.py:54
  912.1 19.7 %custom-call.56 = f32[2,1,128,128]{2,3,1,0:T(8,128)S(1)} custom-call(f32[2,1,128,128]{3,2,1,0:T(8,128)S(1)} %select_bitcast_fusion), custom_call_target="InvertDiagBlocksLowerTriangular" | custom-call | tf_op jit(solution)/shard_map/vmap(jit(cholesky))/cholesky | solution.py:54
  932.5 23.5 %custom-call.57 = f32[2,128,128]{2,1,0:T(8,128)S(1)} custom-call(f32[2,128,128]{2,1,0:T(8,128)S(1)} %convolution_subtract_fusion.6), custom_call_target="Cholesky" | custom-call | tf_op jit(solution)/shard_map/vmap(jit(cholesky))/cholesky | solution.py:54
  960.4 39.6 %custom-call.58 = f32[2,2,128,128]{2,3,1,0:T(8,128)S(1)} custom-call(f32[2,2,128,128]{3,2,1,0:T(8,128)S(1)} %bitcast.1068), custom_call_target="InvertDiagBlocksLowerTriangular" | custom-call | tf_op jit(solution)/shard_map/vmap(jit(_cho_solve))/triangular_solve | solution.py:55
  (633 shorter events, 265.0 us)
Async XLA Ops:
  2.2 147.3 %collective-permute-start.1 = (f32[128,128]{0,1:T(8,128)S(1)}, f32[128,128]{0,1:T(8,128)S(1)}, u32[]{:S(2)}, u32[]{:S(2)}) collective-permute-start(f32[128,128]{0,1:T(8,128)S(1)} %fusion.154), channel_id=1, source_target_pairs={{0,2},{2,4},{4,6},{6,8},{8,10},{10,12},{12,14},{14,16},{16,18},{18... | collective-permute-start | bytes 196616 | tf_op jit(solution)/shard_map/ppermute | solution.py:10
  132.0 20.6 %collective-permute-start.3 = (f32[128,128]{0,1:T(8,128)S(1)}, f32[128,128]{0,1:T(8,128)S(1)}, u32[]{:S(2)}, u32[]{:S(2)}) collective-permute-start(f32[128,128]{0,1:T(8,128)S(1)} %convolution_add_fusion.81), channel_id=1, source_target_pairs={{0,2},{2,4},{4,6},{6,8},{8,10},{10,12},{12,14},{14,16},{16,18},{18... | collective-permute-start | bytes 196616 | tf_op jit(solution)/shard_map/ppermute | solution.py:10
  135.7 19.1 %collective-permute-start = (f32[128,128]{0,1:T(8,128)S(1)}, f32[128,128]{0,1:T(8,128)S(1)}, u32[]{:S(2)}, u32[]{:S(2)}) collective-permute-start(f32[128,128]{0,1:T(8,128)S(1)} %convolution_subtract_fusion.102), channel_id=1, source_target_pairs={{0,2},{2,4},{4,6},{6,8},{8,10},{10,12},{12,14},{14,16},{16,18},{18... | collective-permute-start | bytes 196616 | tf_op jit(solution)/shard_map/ppermute | solution.py:10
  140.2 143.4 %collective-permute-start.7 = (f32[128,128]{0,1:T(8,128)S(1)}, f32[128,128]{0,1:T(8,128)S(1)}, u32[]{:S(2)}, u32[]{:S(2)}) collective-permute-start(f32[128,128]{0,1:T(8,128)S(1)} %fusion.52), channel_id=1, source_target_pairs={{0,2},{2,4},{4,6},{6,8},{8,10},{10,12},{12,14},{14,16},{16,18},{18... | collective-permute-start | bytes 196616 | tf_op jit(solution)/shard_map/ppermute | solution.py:10
  143.9 139.9 %collective-permute-start.6 = (f32[128,128]{0,1:T(8,128)S(1)}, f32[128,128]{0,1:T(8,128)S(1)}, u32[]{:S(2)}, u32[]{:S(2)}) collective-permute-start(f32[128,128]{0,1:T(8,128)S(1)} %fusion.53), channel_id=1, source_target_pairs={{0,2},{2,4},{4,6},{6,8},{8,10},{10,12},{12,14},{14,16},{16,18},{18... | collective-permute-start | bytes 196616 | tf_op jit(solution)/shard_map/ppermute | solution.py:10
  154.7 140.8 %collective-permute-start.11 = (f32[128,128]{0,1:T(8,128)S(1)}, f32[128,128]{0,1:T(8,128)S(1)}, u32[]{:S(2)}, u32[]{:S(2)}) collective-permute-start(f32[128,128]{0,1:T(8,128)S(1)} %fusion.49), channel_id=1, source_target_pairs={{2,0},{4,2},{6,4},{8,6},{10,8},{12,10},{14,12},{16,14},{18,16},{20... | collective-permute-start | bytes 196616 | tf_op jit(solution)/shard_map/ppermute | solution.py:10
  159.8 136.0 %collective-permute-start.10 = (f32[128,128]{0,1:T(8,128)S(1)}, f32[128,128]{0,1:T(8,128)S(1)}, u32[]{:S(2)}, u32[]{:S(2)}) collective-permute-start(f32[128,128]{0,1:T(8,128)S(1)} %fusion.50), channel_id=1, source_target_pairs={{2,0},{4,2},{6,4},{8,6},{10,8},{12,10},{14,12},{16,14},{18,16},{20... | collective-permute-start | bytes 196616 | tf_op jit(solution)/shard_map/ppermute | solution.py:10
  284.0 178.9 %collective-permute-start.18 = (f32[128,128]{1,0:T(8,128)S(1)}, f32[128,128]{1,0:T(8,128)S(1)}, u32[]{:S(2)}, u32[]{:S(2)}) collective-permute-start(f32[128,128]{1,0:T(8,128)S(1)} %fusion.46), channel_id=1, source_target_pairs={{2,0},{4,2},{6,4},{8,6},{10,8},{12,10},{14,12},{16,14},{18,16},{20... | collective-permute-start | bytes 196616 | tf_op jit(solution)/shard_map/ppermute | solution.py:10
  285.6 24.8 %collective-permute-start.14 = (f32[128,128]{0,1:T(8,128)S(1)}, f32[128,128]{0,1:T(8,128)S(1)}, u32[]{:S(2)}, u32[]{:S(2)}) collective-permute-start(f32[128,128]{0,1:T(8,128)S(1)} %convolution_add_fusion.69), channel_id=1, source_target_pairs={{0,2},{2,4},{4,6},{6,8},{8,10},{10,12},{12,14},{14,16},{16,18},{18... | collective-permute-start | bytes 196616 | tf_op jit(solution)/shard_map/ppermute | solution.py:10
  294.0 21.9 %collective-permute-start.15 = (f32[128,128]{0,1:T(8,128)S(1)}, f32[128,128]{0,1:T(8,128)S(1)}, u32[]{:S(2)}, u32[]{:S(2)}) collective-permute-start(f32[128,128]{0,1:T(8,128)S(1)} %convolution_add_fusion.68), channel_id=1, source_target_pairs={{2,0},{4,2},{6,4},{8,6},{10,8},{12,10},{14,12},{16,14},{18,16},{20... | collective-permute-start | bytes 196616 | tf_op jit(solution)/shard_map/ppermute | solution.py:10
  297.7 38.3 %collective-permute-start.16 = (f32[128,128]{0,1:T(8,128)S(1)}, f32[128,128]{0,1:T(8,128)S(1)}, u32[]{:S(2)}, u32[]{:S(2)}) collective-permute-start(f32[128,128]{0,1:T(8,128)S(1)} %convolution_add_fusion.67), channel_id=1, source_target_pairs={{0,2},{2,4},{4,6},{6,8},{8,10},{10,12},{12,14},{14,16},{16,18},{18... | collective-permute-start | bytes 196616 | tf_op jit(solution)/shard_map/ppermute | solution.py:10
  305.2 36.0 %collective-permute-start.17 = (f32[128,128]{0,1:T(8,128)S(1)}, f32[128,128]{0,1:T(8,128)S(1)}, u32[]{:S(2)}, u32[]{:S(2)}) collective-permute-start(f32[128,128]{0,1:T(8,128)S(1)} %convolution_add_fusion.66), channel_id=1, source_target_pairs={{2,0},{4,2},{6,4},{8,6},{10,8},{12,10},{14,12},{16,14},{18,16},{20... | collective-permute-start | bytes 196616 | tf_op jit(solution)/shard_map/ppermute | solution.py:10
  324.6 139.8 %collective-permute-start.9 = (f32[128,128]{1,0:T(8,128)S(1)}, f32[128,128]{1,0:T(8,128)S(1)}, u32[]{:S(2)}, u32[]{:S(2)}) collective-permute-start(f32[128,128]{1,0:T(8,128)S(1)} %fusion.51), channel_id=1, source_target_pairs={{2,0},{4,2},{6,4},{8,6},{10,8},{12,10},{14,12},{16,14},{18,16},{20... | collective-permute-start | bytes 196616 | tf_op jit(solution)/shard_map/ppermute | solution.py:10
  330.7 141.3 %collective-permute-start.21 = (f32[128,128]{1,0:T(8,128)S(1)}, f32[128,128]{1,0:T(8,128)S(1)}, u32[]{:S(2)}, u32[]{:S(2)}) collective-permute-start(f32[128,128]{1,0:T(8,128)S(1)} %fusion.44), channel_id=1, source_target_pairs={{0,2},{2,4},{4,6},{6,8},{8,10},{10,12},{12,14},{14,16},{16,18},{18... | collective-permute-start | bytes 196616 | tf_op jit(solution)/shard_map/ppermute | solution.py:10
  336.0 141.2 %collective-permute-start.20 = (f32[128,128]{1,0:T(8,128)S(1)}, f32[128,128]{1,0:T(8,128)S(1)}, u32[]{:S(2)}, u32[]{:S(2)}) collective-permute-start(f32[128,128]{1,0:T(8,128)S(1)} %fusion.45), channel_id=1, source_target_pairs={{0,2},{2,4},{4,6},{6,8},{8,10},{10,12},{12,14},{14,16},{16,18},{18... | collective-permute-start | bytes 196616 | tf_op jit(solution)/shard_map/ppermute | solution.py:10
  341.2 144.4 %collective-permute-start.24 = (f32[128,128]{1,0:T(8,128)S(1)}, f32[128,128]{1,0:T(8,128)S(1)}, u32[]{:S(2)}, u32[]{:S(2)}) collective-permute-start(f32[128,128]{1,0:T(8,128)S(1)} %fusion.42), channel_id=1, source_target_pairs={{2,0},{4,2},{6,4},{8,6},{10,8},{12,10},{14,12},{16,14},{18,16},{20... | collective-permute-start | bytes 196616 | tf_op jit(solution)/shard_map/ppermute | solution.py:10
  462.9 17.9 %collective-permute-start.25 = (f32[128,128]{1,0:T(8,128)S(1)}, f32[128,128]{1,0:T(8,128)S(1)}, u32[]{:S(2)}, u32[]{:S(2)}) collective-permute-start(f32[128,128]{1,0:T(8,128)S(1)} %fusion.41), channel_id=1, source_target_pairs={{2,0},{4,2},{6,4},{8,6},{10,8},{12,10},{14,12},{16,14},{18,16},{20... | collective-permute-start | bytes 196616 | tf_op jit(solution)/shard_map/ppermute | solution.py:10
  464.4 23.7 %collective-permute-start.28 = (f32[128,128]{1,0:T(8,128)S(1)}, f32[128,128]{1,0:T(8,128)S(1)}, u32[]{:S(2)}, u32[]{:S(2)}) collective-permute-start(f32[128,128]{1,0:T(8,128)S(1)} %fusion.39), channel_id=1, source_target_pairs={{0,2},{2,4},{4,6},{6,8},{8,10},{10,12},{12,14},{14,16},{16,18},{18... | collective-permute-start | bytes 196616 | tf_op jit(solution)/shard_map/ppermute | solution.py:10
  472.1 21.3 %collective-permute-start.27 = (f32[128,128]{1,0:T(8,128)S(1)}, f32[128,128]{1,0:T(8,128)S(1)}, u32[]{:S(2)}, u32[]{:S(2)}) collective-permute-start(f32[128,128]{1,0:T(8,128)S(1)} %fusion.40), channel_id=1, source_target_pairs={{0,2},{2,4},{4,6},{6,8},{8,10},{10,12},{12,14},{14,16},{16,18},{18... | collective-permute-start | bytes 196616 | tf_op jit(solution)/shard_map/ppermute | solution.py:10
  477.5 176.7 %collective-permute-start.34 = (f32[128,128]{1,0:T(8,128)S(1)}, f32[128,128]{1,0:T(8,128)S(1)}, u32[]{:S(2)}, u32[]{:S(2)}) collective-permute-start(f32[128,128]{1,0:T(8,128)S(1)} %fusion.38), channel_id=1, source_target_pairs={{4,0},{6,2},{8,4},{10,6},{12,8},{14,10},{16,12},{18,14},{20,16},{2... | collective-permute-start | bytes 196616 | tf_op jit(solution)/shard_map/ppermute | solution.py:10
  480.8 22.6 %collective-permute-start.30 = (f32[128,128]{0,1:T(8,128)S(1)}, f32[128,128]{0,1:T(8,128)S(1)}, u32[]{:S(2)}, u32[]{:S(2)}) collective-permute-start(f32[128,128]{0,1:T(8,128)S(1)} %convolution_add_fusion.57), channel_id=1, source_target_pairs={{0,4},{2,6},{4,8},{6,10},{8,12},{10,14},{12,16},{14,18},{16,20},{1... | collective-permute-start | bytes 196616 | tf_op jit(solution)/shard_map/ppermute | solution.py:10
  485.6 23.3 %collective-permute-start.31 = (f32[128,128]{0,1:T(8,128)S(1)}, f32[128,128]{0,1:T(8,128)S(1)}, u32[]{:S(2)}, u32[]{:S(2)}) collective-permute-start(f32[128,128]{0,1:T(8,128)S(1)} %convolution_add_fusion.56), channel_id=1, source_target_pairs={{4,0},{6,2},{8,4},{10,6},{12,8},{14,10},{16,12},{18,14},{20,16},{2... | collective-permute-start | bytes 196616 | tf_op jit(solution)/shard_map/ppermute | solution.py:10
  488.1 40.2 %collective-permute-start.32 = (f32[128,128]{0,1:T(8,128)S(1)}, f32[128,128]{0,1:T(8,128)S(1)}, u32[]{:S(2)}, u32[]{:S(2)}) collective-permute-start(f32[128,128]{0,1:T(8,128)S(1)} %convolution_add_fusion.55), channel_id=1, source_target_pairs={{0,4},{2,6},{4,8},{6,10},{8,12},{10,14},{12,16},{14,18},{16,20},{1... | collective-permute-start | bytes 196616 | tf_op jit(solution)/shard_map/ppermute | solution.py:10
  494.6 37.7 %collective-permute-start.33 = (f32[128,128]{0,1:T(8,128)S(1)}, f32[128,128]{0,1:T(8,128)S(1)}, u32[]{:S(2)}, u32[]{:S(2)}) collective-permute-start(f32[128,128]{0,1:T(8,128)S(1)} %convolution_add_fusion.54), channel_id=1, source_target_pairs={{4,0},{6,2},{8,4},{10,6},{12,8},{14,10},{16,12},{18,14},{20,16},{2... | collective-permute-start | bytes 196616 | tf_op jit(solution)/shard_map/ppermute | solution.py:10
  517.9 137.9 %collective-permute-start.23 = (f32[128,128]{1,0:T(8,128)}, f32[128,128]{1,0:T(8,128)S(1)}, u32[]{:S(2)}, u32[]{:S(2)}) collective-permute-start(f32[128,128]{1,0:T(8,128)} %fusion.43), channel_id=1, source_target_pairs={{4,0},{6,2},{8,4},{10,6},{12,8},{14,10},{16,12},{18,14},{20,16},{2... | collective-permute-start | bytes 196616 | tf_op jit(solution)/shard_map/ppermute | solution.py:10
  523.1 138.7 %collective-permute-start.37 = (f32[128,128]{1,0:T(8,128)S(1)}, f32[128,128]{1,0:T(8,128)S(1)}, u32[]{:S(2)}, u32[]{:S(2)}) collective-permute-start(f32[128,128]{1,0:T(8,128)S(1)} %fusion.36), channel_id=1, source_target_pairs={{0,4},{2,6},{4,8},{6,10},{8,12},{10,14},{12,16},{14,18},{16,20},{1... | collective-permute-start | bytes 196616 | tf_op jit(solution)/shard_map/ppermute | solution.py:10
  528.4 138.6 %collective-permute-start.36 = (f32[128,128]{1,0:T(8,128)S(1)}, f32[128,128]{1,0:T(8,128)S(1)}, u32[]{:S(2)}, u32[]{:S(2)}) collective-permute-start(f32[128,128]{1,0:T(8,128)S(1)} %fusion.37), channel_id=1, source_target_pairs={{0,4},{2,6},{4,8},{6,10},{8,12},{10,14},{12,16},{14,18},{16,20},{1... | collective-permute-start | bytes 196616 | tf_op jit(solution)/shard_map/ppermute | solution.py:10
  532.3 138.3 %collective-permute-start.41 = (f32[128,128]{1,0:T(8,128)S(1)}, f32[128,128]{1,0:T(8,128)S(1)}, u32[]{:S(2)}, u32[]{:S(2)}) collective-permute-start(f32[128,128]{1,0:T(8,128)S(1)} %fusion.33), channel_id=1, source_target_pairs={{4,0},{6,2},{8,4},{10,6},{12,8},{14,10},{16,12},{18,14},{20,16},{2... | collective-permute-start | bytes 196616 | tf_op jit(solution)/shard_map/ppermute | solution.py:10
  654.2 21.1 %collective-permute-start.40 = (f32[128,128]{1,0:T(8,128)S(1)}, f32[128,128]{1,0:T(8,128)S(1)}, u32[]{:S(2)}, u32[]{:S(2)}) collective-permute-start(f32[128,128]{1,0:T(8,128)S(1)} %fusion.34), channel_id=1, source_target_pairs={{4,0},{6,2},{8,4},{10,6},{12,8},{14,10},{16,12},{18,14},{20,16},{2... | collective-permute-start | bytes 196616 | tf_op jit(solution)/shard_map/ppermute | solution.py:10
  655.7 26.9 %collective-permute-start.43 = (f32[128,128]{1,0:T(8,128)S(1)}, f32[128,128]{1,0:T(8,128)S(1)}, u32[]{:S(2)}, u32[]{:S(2)}) collective-permute-start(f32[128,128]{1,0:T(8,128)S(1)} %fusion.32), channel_id=1, source_target_pairs={{0,4},{2,6},{4,8},{6,10},{8,12},{10,14},{12,16},{14,18},{16,20},{1... | collective-permute-start | bytes 196616 | tf_op jit(solution)/shard_map/ppermute | solution.py:10
  661.8 16.1 %collective-permute-start.44 = (f32[128,128]{1,0:T(8,128)S(1)}, f32[128,128]{1,0:T(8,128)S(1)}, u32[]{:S(2)}, u32[]{:S(2)}) collective-permute-start(f32[128,128]{1,0:T(8,128)S(1)} %fusion.31), channel_id=1, source_target_pairs={{0,4},{2,6},{4,8},{6,10},{8,12},{10,14},{12,16},{14,18},{16,20},{1... | collective-permute-start | bytes 196616 | tf_op jit(solution)/shard_map/ppermute | solution.py:10
  667.3 170.4 %collective-permute-start.50 = (f32[128,128]{1,0:T(8,128)S(1)}, f32[128,128]{1,0:T(8,128)S(1)}, u32[]{:S(2)}, u32[]{:S(2)}) collective-permute-start(f32[128,128]{1,0:T(8,128)S(1)} %fusion.30), channel_id=1, source_target_pairs={{8,0},{10,2},{12,4},{14,6},{16,8},{18,10},{20,12},{22,14},{24,16},... | collective-permute-start | bytes 196616 | tf_op jit(solution)/shard_map/ppermute | solution.py:10
  670.6 22.1 %collective-permute-start.46 = (f32[128,128]{0,1:T(8,128)S(1)}, f32[128,128]{0,1:T(8,128)S(1)}, u32[]{:S(2)}, u32[]{:S(2)}) collective-permute-start(f32[128,128]{0,1:T(8,128)S(1)} %convolution_add_fusion.45), channel_id=1, source_target_pairs={{0,8},{2,10},{4,12},{6,14},{8,16},{10,18},{12,20},{14,22},{16,24},... | collective-permute-start | bytes 196616 | tf_op jit(solution)/shard_map/ppermute | solution.py:10
  675.4 21.9 %collective-permute-start.47 = (f32[128,128]{0,1:T(8,128)S(1)}, f32[128,128]{0,1:T(8,128)S(1)}, u32[]{:S(2)}, u32[]{:S(2)}) collective-permute-start(f32[128,128]{0,1:T(8,128)S(1)} %convolution_add_fusion.44), channel_id=1, source_target_pairs={{8,0},{10,2},{12,4},{14,6},{16,8},{18,10},{20,12},{22,14},{24,16},... | collective-permute-start | bytes 196616 | tf_op jit(solution)/shard_map/ppermute | solution.py:10
  677.9 35.6 %collective-permute-start.48 = (f32[128,128]{0,1:T(8,128)S(1)}, f32[128,128]{0,1:T(8,128)S(1)}, u32[]{:S(2)}, u32[]{:S(2)}) collective-permute-start(f32[128,128]{0,1:T(8,128)S(1)} %convolution_add_fusion.43), channel_id=1, source_target_pairs={{0,8},{2,10},{4,12},{6,14},{8,16},{10,18},{12,20},{14,22},{16,24},... | collective-permute-start | bytes 196616 | tf_op jit(solution)/shard_map/ppermute | solution.py:10
  683.9 32.3 %collective-permute-start.49 = (f32[128,128]{0,1:T(8,128)S(1)}, f32[128,128]{0,1:T(8,128)S(1)}, u32[]{:S(2)}, u32[]{:S(2)}) collective-permute-start(f32[128,128]{0,1:T(8,128)S(1)} %convolution_add_fusion.42), channel_id=1, source_target_pairs={{8,0},{10,2},{12,4},{14,6},{16,8},{18,10},{20,12},{22,14},{24,16},... | collective-permute-start | bytes 196616 | tf_op jit(solution)/shard_map/ppermute | solution.py:10
  705.3 133.9 %collective-permute-start.39 = (f32[128,128]{1,0:T(8,128)}, f32[128,128]{1,0:T(8,128)S(1)}, u32[]{:S(2)}, u32[]{:S(2)}) collective-permute-start(f32[128,128]{1,0:T(8,128)} %fusion.35), channel_id=1, source_target_pairs={{8,0},{10,2},{12,4},{14,6},{16,8},{18,10},{20,12},{22,14},{24,16},... | collective-permute-start | bytes 196616 | tf_op jit(solution)/shard_map/ppermute | solution.py:10
  709.6 136.0 %collective-permute-start.53 = (f32[128,128]{1,0:T(8,128)S(1)}, f32[128,128]{1,0:T(8,128)S(1)}, u32[]{:S(2)}, u32[]{:S(2)}) collective-permute-start(f32[128,128]{1,0:T(8,128)S(1)} %fusion.28), channel_id=1, source_target_pairs={{0,8},{2,10},{4,12},{6,14},{8,16},{10,18},{12,20},{14,22},{16,24},... | collective-permute-start | bytes 196616 | tf_op jit(solution)/shard_map/ppermute | solution.py:10
  713.5 136.3 %collective-permute-start.52 = (f32[128,128]{1,0:T(8,128)S(1)}, f32[128,128]{1,0:T(8,128)S(1)}, u32[]{:S(2)}, u32[]{:S(2)}) collective-permute-start(f32[128,128]{1,0:T(8,128)S(1)} %fusion.29), channel_id=1, source_target_pairs={{0,8},{2,10},{4,12},{6,14},{8,16},{10,18},{12,20},{14,22},{16,24},... | collective-permute-start | bytes 196616 | tf_op jit(solution)/shard_map/ppermute | solution.py:10
  716.2 137.5 %collective-permute-start.56 = (f32[128,128]{1,0:T(8,128)S(1)}, f32[128,128]{1,0:T(8,128)S(1)}, u32[]{:S(2)}, u32[]{:S(2)}) collective-permute-start(f32[128,128]{1,0:T(8,128)S(1)} %fusion.26), channel_id=1, source_target_pairs={{8,0},{10,2},{12,4},{14,6},{16,8},{18,10},{20,12},{22,14},{24,16},... | collective-permute-start | bytes 196616 | tf_op jit(solution)/shard_map/ppermute | solution.py:10
  837.7 17.5 %collective-permute-start.55 = (f32[128,128]{1,0:T(8,128)S(1)}, f32[128,128]{1,0:T(8,128)S(1)}, u32[]{:S(2)}, u32[]{:S(2)}) collective-permute-start(f32[128,128]{1,0:T(8,128)S(1)} %fusion.27), channel_id=1, source_target_pairs={{8,0},{10,2},{12,4},{14,6},{16,8},{18,10},{20,12},{22,14},{24,16},... | collective-permute-start | bytes 196616 | tf_op jit(solution)/shard_map/ppermute | solution.py:10
  839.2 22.7 %collective-permute-start.59 = (f32[128,128]{1,0:T(8,128)S(1)}, f32[128,128]{1,0:T(8,128)S(1)}, u32[]{:S(2)}, u32[]{:S(2)}) collective-permute-start(f32[128,128]{1,0:T(8,128)S(1)} %fusion.24), channel_id=1, source_target_pairs={{0,8},{2,10},{4,12},{6,14},{8,16},{10,18},{12,20},{14,22},{16,24},... | collective-permute-start | bytes 196616 | tf_op jit(solution)/shard_map/ppermute | solution.py:10
  845.7 16.5 %collective-permute-start.58 = (f32[128,128]{1,0:T(8,128)S(1)}, f32[128,128]{1,0:T(8,128)S(1)}, u32[]{:S(2)}, u32[]{:S(2)}) collective-permute-start(f32[128,128]{1,0:T(8,128)S(1)} %fusion.25), channel_id=1, source_target_pairs={{0,8},{2,10},{4,12},{6,14},{8,16},{10,18},{12,20},{14,22},{16,24},... | collective-permute-start | bytes 196616 | tf_op jit(solution)/shard_map/ppermute | solution.py:10
  849.8 22.9 %collective-permute-start.61 = (f32[128,128]{0,1:T(8,128)S(1)}, f32[128,128]{0,1:T(8,128)S(1)}, u32[]{:S(2)}, u32[]{:S(2)}) collective-permute-start(f32[128,128]{0,1:T(8,128)S(1)} %convolution_add_fusion.33), channel_id=1, source_target_pairs={{0,16},{2,18},{4,20},{6,22},{8,24},{10,26},{12,28},{14,30},{1,17},... | collective-permute-start | bytes 196616 | tf_op jit(solution)/shard_map/ppermute | solution.py:10
  853.7 20.3 %collective-permute-start.62 = (f32[128,128]{0,1:T(8,128)S(1)}, f32[128,128]{0,1:T(8,128)S(1)}, u32[]{:S(2)}, u32[]{:S(2)}) collective-permute-start(f32[128,128]{0,1:T(8,128)S(1)} %convolution_add_fusion.32), channel_id=1, source_target_pairs={{16,0},{18,2},{20,4},{22,6},{24,8},{26,10},{28,12},{30,14},{17,1},... | collective-permute-start | bytes 196616 | tf_op jit(solution)/shard_map/ppermute | solution.py:10
  856.4 30.6 %collective-permute-start.63 = (f32[128,128]{0,1:T(8,128)S(1)}, f32[128,128]{0,1:T(8,128)S(1)}, u32[]{:S(2)}, u32[]{:S(2)}) collective-permute-start(f32[128,128]{0,1:T(8,128)S(1)} %convolution_add_fusion.31), channel_id=1, source_target_pairs={{0,16},{2,18},{4,20},{6,22},{8,24},{10,26},{12,28},{14,30},{1,17},... | collective-permute-start | bytes 196616 | tf_op jit(solution)/shard_map/ppermute | solution.py:10
  863.3 23.7 %collective-permute-start.64 = (f32[128,128]{0,1:T(8,128)S(1)}, f32[128,128]{0,1:T(8,128)S(1)}, u32[]{:S(2)}, u32[]{:S(2)}) collective-permute-start(f32[128,128]{0,1:T(8,128)S(1)} %convolution_add_fusion.30), channel_id=1, source_target_pairs={{16,0},{18,2},{20,4},{22,6},{24,8},{26,10},{28,12},{30,14},{17,1},... | collective-permute-start | bytes 196616 | tf_op jit(solution)/shard_map/ppermute | solution.py:10
  865.2 14.3 %collective-permute-start.51 = (f32[128,128]{0,1:T(8,128)S(1)}, f32[128,128]{0,1:T(8,128)S(1)}, u32[]{:S(2)}, u32[]{:S(2)}) collective-permute-start(f32[128,128]{0,1:T(8,128)S(1)} %convolution_subtract_fusion.57), channel_id=1, source_target_pairs={{0,16},{2,18},{4,20},{6,22},{8,24},{10,26},{12,28},{14,30},{1,17},... | collective-permute-start | bytes 196616 | tf_op jit(solution)/shard_map/ppermute | solution.py:10
  (20 other events, 129.5 us)
where the time goes:
time: 1020 us; the launch traced here: 1010 us
  other arithmetic  640 us (63%)
  starting transfers between devices  197 us (19%)
  matrix products  112 us (11%)
  local copies, waits for them, and re-layouts  28.6 us (3%)
  waiting for transfers between devices  24.7 us (2%)
    another operation x49, other arithmetic, invert_single(): factor = jnp.linalg.cholesky(stacked)  401 us
    another operation x14, other arithmetic, invert_single(): jax.scipy.linalg.cho_solve((factor, True), jnp.concatenate([adjoint[0], a...  238 us
    ppermute x65, starting transfers between devices, passed_along(): return lax.ppermute(block, axis, route)  197 us
    dot_general x324, matrix products, real_product(): jnp.dot(first, second, precision=lax.Precision.HIGHEST, preferred_element...  96.3 us
    ppermute x65, waiting for transfers between devices, passed_along(): return lax.ppermute(block, axis, route)  24.7 us
    another operation x43, local copies, waits for them, and re-layouts, invert_single(): jax.scipy.linalg.cho_solve((factor, True), jnp.concatenate([adjoint[0], a...  24.6 us
  transfers between devices with their start and end apart: 65, of which 14 were waited for; matrix products, arithmetic and copies ran while one was open for 65% of the time, Pallas kernels for 0%

commit v1 on v0

v1 whole, which is shorter than its diff:
```python
import functools

import jax
import jax.numpy as jnp
from jax import lax
from jax.experimental import pallas as pl
from jax.experimental.pallas import tpu as pltpu
from jax.sharding import PartitionSpec as P

REFINEMENTS = 1
TILE = 8


def dot(first, second):
    return jnp.dot(
        first, second, precision=lax.Precision.HIGHEST, preferred_element_type=jnp.float32
    )


def product(first, second):
    columns = second[0].shape[1]
    left = jnp.concatenate([first[0], first[1]], axis=1)
    right = jnp.concatenate(
        [
            jnp.concatenate([second[0], second[1]], axis=1),
            jnp.concatenate([-second[1], second[0]], axis=1),
        ],
        axis=0,
    )
    out = dot(left, right)
    return (out[:, :columns], out[:, columns:])


def flipped(block):
    return (block[0].T, block[1].T)


def rows(*blocks):
    return tuple(jnp.concatenate([b[part] for b in blocks], axis=0) for part in (0, 1))


def cols(*blocks):
    return tuple(jnp.concatenate([b[part] for b in blocks], axis=1) for part in (0, 1))


def chosen(flag, first, second):
    return tuple(jnp.where(flag, a, b) for a, b in zip(first, second))


def read(ref, index=0):
    return (ref[index], ref[index + 1])


def write(ref, block, index=0):
    ref[index] = block[0]
    ref[index + 1] = block[1]


def eye(size):
    row = lax.broadcasted_iota(jnp.int32, (size, size), 0)
    column = lax.broadcasted_iota(jnp.int32, (size, size), 1)
    return row == column


def inverse(block):
    size = block[0].shape[0]
    lane = lax.broadcasted_iota(jnp.int32, (1, size), 1)
    sub = lax.broadcasted_iota(jnp.int32, (TILE, size), 0)

    def trip(_, carried):
        real, imag = carried
        for j in range(TILE):
            pivot_r, pivot_i = real[j : j + 1, j : j + 1], imag[j : j + 1, j : j + 1]
            scale = 1.0 / (pivot_r * pivot_r + pivot_i * pivot_i)
            q_r, q_i = pivot_r * scale, -pivot_i * scale
            row_r, row_i = real[j : j + 1, :], imag[j : j + 1, :]
            here = lane == j
            new_r = jnp.where(here, q_r, row_r * q_r - row_i * q_i)
            new_i = jnp.where(here, q_i, row_r * q_i + row_i * q_r)
            use_r = jnp.where(here, 1.0 + q_r, new_r)
            col_r, col_i = real[:, j : j + 1], imag[:, j : j + 1]
            real, imag = (
                real - (col_r * use_r - col_i * new_i),
                imag - (col_r * new_i + col_i * use_r),
            )
            at = sub == j
            real = jnp.concatenate([jnp.where(at, new_r, real[:TILE]), real[TILE:]], axis=0)
            imag = jnp.concatenate([jnp.where(at, new_i, imag[:TILE]), imag[TILE:]], axis=0)
        real = jnp.concatenate([real[TILE:], real[:TILE]], axis=0)
        imag = jnp.concatenate([imag[TILE:], imag[:TILE]], axis=0)
        return pltpu.roll(real, size - TILE, 1), pltpu.roll(imag, size - TILE, 1)

    estimate = lax.fori_loop(0, size // TILE, trip, block)
    for _ in range(REFINEMENTS):
        residue = product(block, estimate)
        one = jnp.where(eye(size), 1.0, 0.0)
        fix = product(estimate, (one - residue[0], -residue[1]))
        estimate = (estimate[0] + fix[0], estimate[1] + fix[1])
    return estimate


def begin(energy_ref, broad_ref, flags_ref, onsite_ref, mix_ref, hop_ref, hopmix_ref,
          crit_ref, rest_ref, own_ref):
    size = mix_ref.shape[1]
    unit = eye(size)
    diagonal_i = jnp.where(unit, broad_ref[0], 0.0)

    def onsite(k):
        mixing = mix_ref[k]
        diagonal = jnp.where(unit, energy_ref[0] - onsite_ref[k : k + 1, :], 0.0)
        return diagonal - 0.5 * (mixing + mixing.T)

    def coupling(k):
        return jnp.where(unit, hop_ref[k : k + 1, :], 0.0) + hopmix_ref[k]

    lower = coupling(0)
    upper = jnp.where(flags_ref[0] > 0, 0.0, coupling(1))
    middle = inverse((onsite(1), diagonal_i))
    legs = jnp.concatenate([lower.T, upper], axis=1)
    weighted = dot(jnp.concatenate([middle[0], middle[1]], axis=0), legs)
    to_low = (weighted[:size, :size], weighted[size:, :size])
    to_high = (weighted[:size, size:], weighted[size:, size:])
    both = jnp.concatenate(
        [to_low[0], to_low[1], to_high[0], to_high[1]], axis=1
    )
    outs = dot(jnp.concatenate([lower, upper.T], axis=0), both)
    alpha = (onsite(0) - outs[:size, :size], diagonal_i - outs[:size, size : 2 * size])
    link = (outs[:size, 2 * size : 3 * size], outs[:size, 3 * size :])
    beta = (outs[size:, 2 * size : 3 * size], outs[size:, 3 * size :])
    is_high = flags_ref[1] > 0
    write(crit_ref, chosen(is_high, alpha, beta))
    write(rest_ref, link)
    write(rest_ref, chosen(is_high, beta, alpha), 2)
    write(own_ref, middle)
    write(own_ref, to_low, 2)
    write(own_ref, to_high, 4)


def eliminate(flags_ref, mine_ref, other_ref, y_ref):
    mine, other = read(mine_ref), read(other_ref)
    sign = jnp.where(flags_ref[0] > 0, 1.0, -1.0)
    write(y_ref, inverse((sign * (mine[0] - other[0]), sign * (mine[1] - other[1]))))


def merge(flags_ref, y_ref, mine_ref, other_ref, crit_ref, rest_ref):
    size = y_ref.shape[1]
    high = flags_ref[0] > 0
    next_high = flags_ref[1] > 0
    mine_link, other_link = read(mine_ref), read(other_ref)
    mine_rest, other_rest = read(mine_ref, 2), read(other_ref, 2)
    low_link = chosen(high, other_link, mine_link)
    high_link = chosen(high, mine_link, other_link)
    alpha = chosen(high, other_rest, mine_rest)
    beta = chosen(high, mine_rest, other_rest)
    weighted = product(rows(low_link, flipped(high_link)), read(y_ref))
    outs = product(weighted, cols(flipped(low_link), high_link))
    alpha = tuple(a - o[:size, :size] for a, o in zip(alpha, outs))
    link = tuple(o[:size, size:] for o in outs)
    beta = tuple(b + o[size:, size:] for b, o in zip(beta, outs))
    write(crit_ref, chosen(next_high, alpha, beta))
    write(rest_ref, link)
    write(rest_ref, chosen(next_high, beta, alpha), 2)


def follow(flags_ref, y_ref, mine_ref, other_ref, first_ref, second_ref, first_out, second_out):
    size = y_ref.shape[1]
    high = flags_ref[0] > 0
    mine_link, other_link = read(mine_ref), read(other_ref)
    low_link = chosen(high, other_link, mine_link)
    high_link = chosen(high, mine_link, other_link)
    states = [[read(ref, 2 * k) for k in range(3)] for ref in (first_ref, second_ref)]
    used = [chosen(high, state[1], state[2]) for state in states]
    weighted = product(rows(*used), read(y_ref))
    legs = product(weighted, cols(flipped(low_link), high_link))
    zero = jnp.zeros((size, size), jnp.float32)
    for k, (state, out) in enumerate(zip(states, (first_out, second_out))):
        part = slice(k * size, (k + 1) * size)
        own = product((weighted[0][part], weighted[1][part]), flipped(used[k]))
        write(out, (state[0][0] + own[0], state[0][1] + own[1]))
        down = tuple(
            jnp.where(high, zero, s) + leg[part, :size] for s, leg in zip(state[1], legs)
        )
        up = tuple(
            jnp.where(high, s, zero) + leg[part, size:] for s, leg in zip(state[2], legs)
        )
        write(out, down, 2)
        write(out, up, 4)


def finish(alpha_ref, first_ref, second_ref, real_ref, imag_ref):
    size = alpha_ref.shape[1]
    top = inverse(read(alpha_ref))
    states = [[read(ref, 2 * k) for k in range(2)] for ref in (first_ref, second_ref)]
    weighted = product(rows(states[0][1], states[1][1]), top)
    for k, state in enumerate(states):
        part = slice(k * size, (k + 1) * size)
        own = product((weighted[0][part], weighted[1][part]), flipped(state[1]))
        real_ref[k] = state[0][0] + own[0]
        imag_ref[k] = state[0][1] + own[1]


VMEM = pl.BlockSpec(memory_space=pltpu.VMEM)
SMEM = pl.BlockSpec(memory_space=pltpu.SMEM)


def launch(body, scalars, arrays, shapes, flops):
    cost = pl.CostEstimate(flops=flops, bytes_accessed=1 << 20, transcendentals=0)
    return pl.pallas_call(
        body,
        out_shape=[jax.ShapeDtypeStruct(s, jnp.float32) for s in shapes],
        in_specs=[SMEM] * len(scalars) + [VMEM] * len(arrays),
        out_specs=[VMEM] * len(shapes),
        cost_estimate=cost,
        name=body.__name__,
    )(*scalars, *arrays)


INVERSE_FLOPS = 5 * 10**9
SMALL_FLOPS = 10**9


def shards(onsite_energy, onsite_mixing, hop_strength, hop_mixing, energy, broadening):
    size = onsite_mixing.shape[1]
    count = lax.axis_size("slab")
    levels = count.bit_length() - 1
    position = lax.axis_index("slab")

    def bit(level):
        if level >= levels:
            return jnp.int32(1)
        return ((position >> level) & 1).astype(jnp.int32)

    is_last = (position == count - 1).astype(jnp.int32)
    crit, rest, second = launch(
        begin,
        (energy, broadening, jnp.stack([is_last, bit(0)])),
        (onsite_energy, onsite_mixing, hop_strength, hop_mixing),
        ((2, size, size), (4, size, size), (6, size, size)),
        INVERSE_FLOPS,
    )
    one = jnp.eye(size, dtype=jnp.float32)
    zero = jnp.zeros((size, size), jnp.float32)
    first = jnp.stack([zero, zero, one, zero, zero, zero])
    for level in range(levels):
        flags = jnp.stack([bit(level), bit(level + 1)])
        pairs = [(i, i ^ (1 << level)) for i in range(count)]
        crit_other = lax.ppermute(crit, "slab", pairs)
        if level == levels - 1:
            pairs = [(i, j) for i, j in pairs if i < j]
        rest_other = lax.ppermute(rest, "slab", pairs)
        (y,) = launch(eliminate, (flags,), (crit, crit_other), ((2, size, size),), INVERSE_FLOPS)
        mine = rest
        crit, rest = launch(
            merge, (flags,), (y, mine, rest_other),
            ((2, size, size), (4, size, size)), SMALL_FLOPS,
        )
        first, second = launch(
            follow, (flags,), (y, mine, rest_other, first, second),
            ((6, size, size), (6, size, size)), SMALL_FLOPS,
        )
    real, imag = launch(
        finish, (), (crit, first, second), ((2, size, size), (2, size, size)), INVERSE_FLOPS
    )
    return real, imag


def solution(mesh):
    return jax.shard_map(
        shards,
        mesh=mesh,
        in_specs=(
            P("slab", None),
            P("slab", None, None),
            P("slab", None),
            P("slab", None, None),
            P("energy"),
            P("energy"),
        ),
        out_specs=(P(("energy", "slab"), None, None), P(("energy", "slab"), None, None)),
        check_vma=False,
    )
```

time: 1020 us -> 159 us (0.16); the launches traced: 1010 us -> 158 us
  other arithmetic: 640 us -> 4.02 us
  starting transfers between devices: 197 us -> 12.3 us
  Pallas kernels: 0 us -> 128 us
  matrix products: 112 us -> 0 us
  local copies, waits for them, and re-layouts: 28.6 us -> 5.57 us
  waiting for transfers between devices: 24.7 us -> 6.49 us
    another operation x76 -> x6, other arithmetic: 639 us -> 4.01 us  [the longest x4 2.52 us: shards(): flags = jnp.stack([bit(level), bit(level + 1)])]
    ppermute x65 -> x8, starting transfers between devices: 197 us -> 12.3 us  [the longest x4 10.2 us: shards(): crit_other = lax.ppermute(crit, 'slab', pairs)]
    pallas_call x0 -> x14, Pallas kernels: none -> 128 us  [launch(): pl.pallas_call(body, out_shape=[jax.ShapeDtypeStruct(s, jnp.float32) for...]
    dot_general x324 -> x0, matrix products: 96.3 us -> none  [real_product(): jnp.dot(first, second, precision=lax.Precision.HIGHEST, preferred_element...]
    another operation x55 -> x2, local copies, waits for them, and re-layouts: 24.9 us -> 0.08 us  [the longest x1 0.07 us: shards(): first = jnp.stack([zero, zero, one, zero, zero, zero])]
    ppermute x65 -> x8, waiting for transfers between devices: 24.7 us -> 6.49 us  [the longest x4 6.48 us: shards(): crit_other = lax.ppermute(crit, 'slab', pairs)]
    another operation x48 -> x0, matrix products: 15.7 us -> none  [the longest x36 11.8 us: invert_single(): jax.scipy.linalg.cho_solve((factor, True), jnp.concatenate([adjoint[0], a...]
  transfers between devices with their start and end apart: 65 -> 8, of which waited for: 14 -> 3; matrix products, arithmetic and copies ran while one was open for 65% -> 2% of each run, Pallas kernels for 0% -> 49%
where the time goes in v1:
time: 159 us; the launch traced here: 158 us
  Pallas kernels  128 us (81%)
  starting transfers between devices  12.3 us (8%)
  waiting for transfers between devices  6.49 us (4%)
  local copies, waits for them, and re-layouts  5.57 us (4%)
  other arithmetic  4.02 us (3%)
  between operations  1.97 us (1%)
    pallas_call x14, Pallas kernels, launch(): pl.pallas_call(body, out_shape=[jax.ShapeDtypeStruct(s, jnp.float32) for...  128 us
    ppermute x4, starting transfers between devices, shards(): crit_other = lax.ppermute(crit, 'slab', pairs)  10.2 us
    ppermute x4, waiting for transfers between devices, shards(): crit_other = lax.ppermute(crit, 'slab', pairs)  6.48 us
    unnamed x20, local copies, waits for them, and re-layouts  5.49 us
  transfers between devices with their start and end apart: 8, of which 3 were waited for; matrix products, arithmetic and copies ran while one was open for 2% of the time, Pallas kernels for 49%

profile of v1, /device:TPU:0, one launch (start us, length us, event | category | flops | bytes accessed | tf_op | source)
XLA Modules:
  0.0 158.4 jit_solution(14469918877654467615)
XLA Ops:
  1.9 0.7 pad_add_fusion.4.flags_ref
  2.6 17.9 %begin.1 = (f32[2,128,128]{2,1,0:T(8,128)}, f32[4,128,128]{2,1,0:T(8,128)}, f32[6,128,128]{2,1,0:T(8,128)}) custom-call(f32[1]{0:T(128)S(6)} %copy.8.energy_ref, f32[1]{0:T(128)S(6)} %copy.9.broad_ref, s32[2]{0:T(128)} %pad_add_fusion.4.flags_ref, f32[2,128]{1,0:T(2,128)} %onsite_ref.1, f32[2,128,128]{2,1,0:T(8,128)} %mix_ref.1, f32[2,128]{1,0:T(2,128)} %hop_ref.1, ...), custom_call_target="tpu_custom_call" | custom-call | flops 5000000000 | bytes 1048576 | tf_op jit(solution)/shard_map/begin/pallas_call | solution.py:208
  20.5 3.0 %collective-permute-start = (f32[2,128,128]{2,1,0:T(8,128)}, f32[2,128,128]{2,1,0:T(8,128)S(1)}, u32[]{:S(2)}, u32[]{:S(2)}) collective-permute-start(f32[2,128,128]{2,1,0:T(8,128)} %get-tuple-element.20.mine_ref), channel_id=1, source_target_pairs={{0,2},{2,0},{4,6},{6,4},{8,10},{10,8},{12,14},{14,12},{16,18},{18,... | collective-permute-start | bytes 393224 | tf_op jit(solution)/shard_map/ppermute | solution.py:247
  23.5 0.0 collective-permute-start.1
  23.5 0.1 pad.2.clone
  23.6 0.8 pad_maximum_fusion.first_ref
  24.4 0.6 pad_add_fusion.3.flags_ref
  25.1 3.0 %collective-permute-done.other_ref = f32[2,128,128]{2,1,0:T(8,128)S(1)} collective-permute-done((f32[2,128,128]{2,1,0:T(8,128)}, f32[2,128,128]{2,1,0:T(8,128)S(1)}, u32[]{:S(2)}, u32[]{:S(2)}) %collective-permute-start) | collective-permute-done | bytes 131104 | tf_op jit(solution)/shard_map/ppermute | solution.py:247
  28.0 0.0 copy-start.7
  28.0 0.7 copy-done.7
  28.7 16.7 %eliminate.4.y_ref = f32[2,128,128]{2,1,0:T(8,128)} custom-call(s32[2]{0:T(128)} %pad_add_fusion.3.flags_ref, f32[2,128,128]{2,1,0:T(8,128)} %get-tuple-element.20.mine_ref, f32[2,128,128]{2,1,0:T(8,128)} %copy-done.7), custom_call_target="tpu_custom_call" | custom-call | flops 5000000000 | bytes 1048576 | tf_op jit(solution)/shard_map/eliminate/pallas_call | solution.py:208
  45.4 0.0 collective-permute-done.1.other_ref
  45.4 0.7 copy-done
  46.1 2.7 %merge.4 = (f32[2,128,128]{2,1,0:T(8,128)}, f32[4,128,128]{2,1,0:T(8,128)}) custom-call(s32[2]{0:T(128)} %pad_add_fusion.3.flags_ref, f32[2,128,128]{2,1,0:T(8,128)} %eliminate.4.y_ref, f32[4,128,128]{2,1,0:T(8,128)} %get-tuple-element.21.mine_ref, f32[4,128,128]{2,1,0:T(8,128)} %copy-done), custom_call_target="tpu_custom_call" | custom-call | flops 1000000000 | bytes 1048576 | tf_op jit(solution)/shard_map/merge/pallas_call | solution.py:208
  48.9 2.0 %collective-permute-start.2 = (f32[2,128,128]{2,1,0:T(8,128)}, f32[2,128,128]{2,1,0:T(8,128)S(1)}, u32[]{:S(2)}, u32[]{:S(2)}) collective-permute-start(f32[2,128,128]{2,1,0:T(8,128)} %get-tuple-element.22.mine_ref), channel_id=1, source_target_pairs={{0,4},{2,6},{4,0},{6,2},{8,12},{10,14},{12,8},{14,10},{16,20},{18,... | collective-permute-start | bytes 393224 | tf_op jit(solution)/shard_map/ppermute | solution.py:247
  50.9 0.7 pad_add_fusion.2.flags_ref
  51.6 0.6 pad_add_fusion.1.flags_ref
  52.2 0.0 collective-permute-start.3
  52.2 3.3 %collective-permute-done.2.other_ref = f32[2,128,128]{2,1,0:T(8,128)S(1)} collective-permute-done((f32[2,128,128]{2,1,0:T(8,128)}, f32[2,128,128]{2,1,0:T(8,128)S(1)}, u32[]{:S(2)}, u32[]{:S(2)}) %collective-permute-start.2) | collective-permute-done | bytes 131104 | tf_op jit(solution)/shard_map/ppermute | solution.py:247
  55.5 0.7 copy-done.9
  56.1 16.7 %eliminate.5.y_ref = f32[2,128,128]{2,1,0:T(8,128)} custom-call(s32[2]{0:T(128)} %pad_add_fusion.2.flags_ref, f32[2,128,128]{2,1,0:T(8,128)} %get-tuple-element.22.mine_ref, f32[2,128,128]{2,1,0:T(8,128)} %copy-done.9), custom_call_target="tpu_custom_call" | custom-call | flops 5000000000 | bytes 1048576 | tf_op jit(solution)/shard_map/eliminate/pallas_call | solution.py:208
  72.9 0.0 collective-permute-done.3.other_ref
  72.9 0.7 copy-done.2
  73.6 2.7 %merge.5 = (f32[2,128,128]{2,1,0:T(8,128)}, f32[4,128,128]{2,1,0:T(8,128)}) custom-call(s32[2]{0:T(128)} %pad_add_fusion.2.flags_ref, f32[2,128,128]{2,1,0:T(8,128)} %eliminate.5.y_ref, f32[4,128,128]{2,1,0:T(8,128)} %get-tuple-element.23.mine_ref, f32[4,128,128]{2,1,0:T(8,128)} %copy-done.2), custom_call_target="tpu_custom_call" | custom-call | flops 1000000000 | bytes 1048576 | tf_op jit(solution)/shard_map/merge/pallas_call | solution.py:208
  76.3 2.1 %collective-permute-start.4 = (f32[2,128,128]{2,1,0:T(8,128)}, f32[2,128,128]{2,1,0:T(8,128)S(1)}, u32[]{:S(2)}, u32[]{:S(2)}) collective-permute-start(f32[2,128,128]{2,1,0:T(8,128)} %get-tuple-element.24.mine_ref), channel_id=1, source_target_pairs={{0,8},{2,10},{4,12},{6,14},{8,0},{10,2},{12,4},{14,6},{16,24},{18,... | collective-permute-start | bytes 393224 | tf_op jit(solution)/shard_map/ppermute | solution.py:247
  78.4 0.6 pad_add_fusion.flags_ref
  79.1 3.6 %follow.4 = (f32[6,128,128]{2,1,0:T(8,128)}, f32[6,128,128]{2,1,0:T(8,128)}) custom-call(s32[2]{0:T(128)} %pad_add_fusion.3.flags_ref, f32[2,128,128]{2,1,0:T(8,128)} %eliminate.4.y_ref, f32[4,128,128]{2,1,0:T(8,128)} %get-tuple-element.21.mine_ref, f32[4,128,128]{2,1,0:T(8,128)} %copy-done, f32[6,128,128]{2,1,0:T(8,128)} %pad_maximum_fusion.first_ref, ...), custom_call_target="tpu_custom_call" | custom-call | flops 1000000000 | bytes 1048576 | tf_op jit(solution)/shard_map/follow/pallas_call | solution.py:208
  82.7 0.0 copy-done.1
  82.7 0.0 collective-permute-start.5
  82.7 0.2 collective-permute-done.4.other_ref
  82.9 0.7 copy-done.8
  83.5 16.7 %eliminate.6.y_ref = f32[2,128,128]{2,1,0:T(8,128)} custom-call(s32[2]{0:T(128)} %pad_add_fusion.1.flags_ref, f32[2,128,128]{2,1,0:T(8,128)} %get-tuple-element.24.mine_ref, f32[2,128,128]{2,1,0:T(8,128)} %copy-done.8), custom_call_target="tpu_custom_call" | custom-call | flops 5000000000 | bytes 1048576 | tf_op jit(solution)/shard_map/eliminate/pallas_call | solution.py:208
  100.2 0.0 collective-permute-done.5.other_ref
  100.2 0.7 copy-done.4
  101.0 2.7 %merge.6 = (f32[2,128,128]{2,1,0:T(8,128)}, f32[4,128,128]{2,1,0:T(8,128)}) custom-call(s32[2]{0:T(128)} %pad_add_fusion.1.flags_ref, f32[2,128,128]{2,1,0:T(8,128)} %eliminate.6.y_ref, f32[4,128,128]{2,1,0:T(8,128)} %get-tuple-element.25.mine_ref, f32[4,128,128]{2,1,0:T(8,128)} %copy-done.4), custom_call_target="tpu_custom_call" | custom-call | flops 1000000000 | bytes 1048576 | tf_op jit(solution)/shard_map/merge/pallas_call | solution.py:208
  103.7 3.1 %collective-permute-start.6 = (f32[2,128,128]{2,1,0:T(8,128)}, f32[2,128,128]{2,1,0:T(8,128)S(1)}, u32[]{:S(2)}, u32[]{:S(2)}) collective-permute-start(f32[2,128,128]{2,1,0:T(8,128)} %get-tuple-element.26.mine_ref), channel_id=1, source_target_pairs={{0,16},{2,18},{4,20},{6,22},{8,24},{10,26},{12,28},{14,30},{16,0},... | collective-permute-start | bytes 393224 | tf_op jit(solution)/shard_map/ppermute | solution.py:247
  106.8 3.6 %follow.5 = (f32[6,128,128]{2,1,0:T(8,128)}, f32[6,128,128]{2,1,0:T(8,128)}) custom-call(s32[2]{0:T(128)} %pad_add_fusion.2.flags_ref, f32[2,128,128]{2,1,0:T(8,128)} %eliminate.5.y_ref, f32[4,128,128]{2,1,0:T(8,128)} %get-tuple-element.23.mine_ref, f32[4,128,128]{2,1,0:T(8,128)} %copy-done.2, f32[6,128,128]{2,1,0:T(8,128)} %get-tuple-element.30.first_ref, ...), custom_call_target="tpu_custom_call" | custom-call | flops 1000000000 | bytes 1048576 | tf_op jit(solution)/shard_map/follow/pallas_call | solution.py:208
  110.4 0.0 copy-done.3
  110.4 2.1 %collective-permute-start.7 = (f32[4,128,128]{2,1,0:T(8,128)S(1)}, f32[4,128,128]{2,1,0:T(8,128)S(1)}, u32[]{:S(2)}, u32[]{:S(2)}) collective-permute-start(f32[4,128,128]{2,1,0:T(8,128)S(1)} %copy-done.3), channel_id=1, source_target_pairs={{0,16},{2,18},{4,20},{6,22},{8,24},{10,26},{12,28},{14,30},{1,17},... | collective-permute-start | bytes 786440 | tf_op jit(solution)/shard_map/ppermute | solution.py:250
  112.5 3.5 %follow.6 = (f32[6,128,128]{2,1,0:T(8,128)}, f32[6,128,128]{2,1,0:T(8,128)}) custom-call(s32[2]{0:T(128)} %pad_add_fusion.1.flags_ref, f32[2,128,128]{2,1,0:T(8,128)} %eliminate.6.y_ref, f32[4,128,128]{2,1,0:T(8,128)} %get-tuple-element.25.mine_ref, f32[4,128,128]{2,1,0:T(8,128)} %copy-done.4, f32[6,128,128]{2,1,0:T(8,128)} %get-tuple-element.32.first_ref, ...), custom_call_target="tpu_custom_call" | custom-call | flops 1000000000 | bytes 1048576 | tf_op jit(solution)/shard_map/follow/pallas_call | solution.py:208
  116.0 0.0 collective-permute-done.6.other_ref
  116.0 0.7 copy-done.6
  116.7 16.7 %eliminate.7.y_ref = f32[2,128,128]{2,1,0:T(8,128)} custom-call(s32[2]{0:T(128)} %pad_add_fusion.flags_ref, f32[2,128,128]{2,1,0:T(8,128)} %get-tuple-element.26.mine_ref, f32[2,128,128]{2,1,0:T(8,128)} %copy-done.6), custom_call_target="tpu_custom_call" | custom-call | flops 5000000000 | bytes 1048576 | tf_op jit(solution)/shard_map/eliminate/pallas_call | solution.py:208
  133.4 0.0 collective-permute-done.7.other_ref
  133.4 0.7 copy-done.5
  134.1 2.8 %merge.7 = (f32[2,128,128]{2,1,0:T(8,128)}, f32[4,128,128]{2,1,0:T(8,128)}) custom-call(s32[2]{0:T(128)} %pad_add_fusion.flags_ref, f32[2,128,128]{2,1,0:T(8,128)} %eliminate.7.y_ref, f32[4,128,128]{2,1,0:T(8,128)} %get-tuple-element.27.mine_ref, f32[4,128,128]{2,1,0:T(8,128)} %copy-done.5), custom_call_target="tpu_custom_call" | custom-call | flops 1000000000 | bytes 1048576 | tf_op jit(solution)/shard_map/merge/pallas_call | solution.py:208
  136.9 3.6 %follow.7 = (f32[6,128,128]{2,1,0:T(8,128)}, f32[6,128,128]{2,1,0:T(8,128)}) custom-call(s32[2]{0:T(128)} %pad_add_fusion.flags_ref, f32[2,128,128]{2,1,0:T(8,128)} %eliminate.7.y_ref, f32[4,128,128]{2,1,0:T(8,128)} %get-tuple-element.27.mine_ref, f32[4,128,128]{2,1,0:T(8,128)} %copy-done.5, f32[6,128,128]{2,1,0:T(8,128)} %get-tuple-element.34.first_ref, ...), custom_call_target="tpu_custom_call" | custom-call | flops 1000000000 | bytes 1048576 | tf_op jit(solution)/shard_map/follow/pallas_call | solution.py:208
  140.4 18.0 %finish.1 = (f32[2,128,128]{2,1,0:T(8,128)}, f32[2,128,128]{2,1,0:T(8,128)}) custom-call(f32[2,128,128]{2,1,0:T(8,128)} %get-tuple-element.28.alpha_ref, f32[6,128,128]{2,1,0:T(8,128)} %get-tuple-element.36.first_ref, f32[6,128,128]{2,1,0:T(8,128)} %get-tuple-element.37.second_ref), custom_call_target="tpu_custom_call" | custom-call | flops 5000000000 | bytes 1048576 | tf_op jit(solution)/shard_map/finish/pallas_call | solution.py:208
  (11 shorter events, 0.0 us)
Async XLA Ops:
  20.5 7.5 %collective-permute-start = (f32[2,128,128]{2,1,0:T(8,128)}, f32[2,128,128]{2,1,0:T(8,128)S(1)}, u32[]{:S(2)}, u32[]{:S(2)}) collective-permute-start(f32[2,128,128]{2,1,0:T(8,128)} %get-tuple-element.20.mine_ref), channel_id=1, source_target_pairs={{0,2},{2,0},{4,6},{6,4},{8,10},{10,8},{12,14},{14,12},{16,18},{18,... | collective-permute-start | bytes 393224 | tf_op jit(solution)/shard_map/ppermute | solution.py:247
  23.5 21.9 %collective-permute-start.1 = (f32[4,128,128]{2,1,0:T(8,128)}, f32[4,128,128]{2,1,0:T(8,128)S(1)}, u32[]{:S(2)}, u32[]{:S(2)}) collective-permute-start(f32[4,128,128]{2,1,0:T(8,128)} %get-tuple-element.21.mine_ref), channel_id=1, source_target_pairs={{0,2},{2,0},{4,6},{6,4},{8,10},{10,8},{12,14},{14,12},{16,18},{18,... | collective-permute-start | bytes 786440 | tf_op jit(solution)/shard_map/ppermute | solution.py:250
  28.0 0.7 copy-start.7
  45.4 0.7 copy-start
  48.9 6.6 %collective-permute-start.2 = (f32[2,128,128]{2,1,0:T(8,128)}, f32[2,128,128]{2,1,0:T(8,128)S(1)}, u32[]{:S(2)}, u32[]{:S(2)}) collective-permute-start(f32[2,128,128]{2,1,0:T(8,128)} %get-tuple-element.22.mine_ref), channel_id=1, source_target_pairs={{0,4},{2,6},{4,0},{6,2},{8,12},{10,14},{12,8},{14,10},{16,20},{18,... | collective-permute-start | bytes 393224 | tf_op jit(solution)/shard_map/ppermute | solution.py:247
  52.2 20.7 %collective-permute-start.3 = (f32[4,128,128]{2,1,0:T(8,128)}, f32[4,128,128]{2,1,0:T(8,128)S(1)}, u32[]{:S(2)}, u32[]{:S(2)}) collective-permute-start(f32[4,128,128]{2,1,0:T(8,128)} %get-tuple-element.23.mine_ref), channel_id=1, source_target_pairs={{0,4},{2,6},{4,0},{6,2},{8,12},{10,14},{12,8},{14,10},{16,20},{18,... | collective-permute-start | bytes 786440 | tf_op jit(solution)/shard_map/ppermute | solution.py:250
  55.5 0.7 copy-start.9
  72.9 0.7 copy-start.2
  76.3 6.6 %collective-permute-start.4 = (f32[2,128,128]{2,1,0:T(8,128)}, f32[2,128,128]{2,1,0:T(8,128)S(1)}, u32[]{:S(2)}, u32[]{:S(2)}) collective-permute-start(f32[2,128,128]{2,1,0:T(8,128)} %get-tuple-element.24.mine_ref), channel_id=1, source_target_pairs={{0,8},{2,10},{4,12},{6,14},{8,0},{10,2},{12,4},{14,6},{16,24},{18,... | collective-permute-start | bytes 393224 | tf_op jit(solution)/shard_map/ppermute | solution.py:247
  79.1 3.6 %copy-start.1 = (f32[4,128,128]{2,1,0:T(8,128)S(1)}, f32[4,128,128]{2,1,0:T(8,128)}, u32[]{:S(2)}) copy-start(f32[4,128,128]{2,1,0:T(8,128)} %get-tuple-element.25.mine_ref) | copy-start | bytes 786436
  82.7 17.6 %collective-permute-start.5 = (f32[4,128,128]{2,1,0:T(8,128)S(1)}, f32[4,128,128]{2,1,0:T(8,128)S(1)}, u32[]{:S(2)}, u32[]{:S(2)}) collective-permute-start(f32[4,128,128]{2,1,0:T(8,128)S(1)} %copy-done.1), channel_id=1, source_target_pairs={{0,8},{2,10},{4,12},{6,14},{8,0},{10,2},{12,4},{14,6},{16,24},{18,... | collective-permute-start | bytes 786440 | tf_op jit(solution)/shard_map/ppermute | solution.py:250
  82.9 0.7 copy-start.8
  100.2 0.7 copy-start.4
  103.7 12.3 %collective-permute-start.6 = (f32[2,128,128]{2,1,0:T(8,128)}, f32[2,128,128]{2,1,0:T(8,128)S(1)}, u32[]{:S(2)}, u32[]{:S(2)}) collective-permute-start(f32[2,128,128]{2,1,0:T(8,128)} %get-tuple-element.26.mine_ref), channel_id=1, source_target_pairs={{0,16},{2,18},{4,20},{6,22},{8,24},{10,26},{12,28},{14,30},{16,0},... | collective-permute-start | bytes 393224 | tf_op jit(solution)/shard_map/ppermute | solution.py:247
  106.8 3.6 %copy-start.3 = (f32[4,128,128]{2,1,0:T(8,128)S(1)}, f32[4,128,128]{2,1,0:T(8,128)}, u32[]{:S(2)}) copy-start(f32[4,128,128]{2,1,0:T(8,128)} %get-tuple-element.27.mine_ref) | copy-start | bytes 786436
  110.4 23.0 %collective-permute-start.7 = (f32[4,128,128]{2,1,0:T(8,128)S(1)}, f32[4,128,128]{2,1,0:T(8,128)S(1)}, u32[]{:S(2)}, u32[]{:S(2)}) collective-permute-start(f32[4,128,128]{2,1,0:T(8,128)S(1)} %copy-done.3), channel_id=1, source_target_pairs={{0,16},{2,18},{4,20},{6,22},{8,24},{10,26},{12,28},{14,30},{1,17},... | collective-permute-start | bytes 786440 | tf_op jit(solution)/shard_map/ppermute | solution.py:250
  116.0 0.7 copy-start.6
  133.4 0.7 copy-start.5

commit v2 on v1

v2 whole, which is shorter than its diff:
```python
import functools

import jax
import jax.numpy as jnp
from jax import lax
from jax.experimental import pallas as pl
from jax.experimental.pallas import tpu as pltpu
from jax.sharding import PartitionSpec as P

TILE = 8


def dot(first, second, precision=lax.Precision.HIGHEST):
    return jnp.dot(first, second, precision=precision, preferred_element_type=jnp.float32)


def product(first, second, precision=lax.Precision.HIGHEST):
    columns = second[0].shape[1]
    left = jnp.concatenate([first[0], first[1]], axis=1)
    right = jnp.concatenate(
        [
            jnp.concatenate([second[0], second[1]], axis=1),
            jnp.concatenate([-second[1], second[0]], axis=1),
        ],
        axis=0,
    )
    out = dot(left, right, precision)
    return (out[:, :columns], out[:, columns:])


def flipped(block):
    return (block[0].T, block[1].T)


def rows(*blocks):
    return tuple(jnp.concatenate([b[part] for b in blocks], axis=0) for part in (0, 1))


def cols(*blocks):
    return tuple(jnp.concatenate([b[part] for b in blocks], axis=1) for part in (0, 1))


def chosen(flag, first, second):
    return tuple(jnp.where(flag, a, b) for a, b in zip(first, second))


def read(ref, *index):
    return (ref[(*index[:-1], index[-1])], ref[(*index[:-1], index[-1] + 1)])


def write(ref, block, *index):
    ref[(*index[:-1], index[-1])] = block[0]
    ref[(*index[:-1], index[-1] + 1)] = block[1]


def eye(size):
    row = lax.broadcasted_iota(jnp.int32, (size, size), 0)
    column = lax.broadcasted_iota(jnp.int32, (size, size), 1)
    return row == column


def times(first_r, first_i, second_r, second_i):
    return (first_r * second_r - first_i * second_i, first_r * second_i + first_i * second_r)


def reciprocal(value):
    guess = pltpu.reciprocal(value, approx=True)
    guess = guess * (2.0 - value * guess)
    return guess * (2.0 - value * guess)


def inverse(block):
    size = block[0].shape[0]
    lane = lax.broadcasted_iota(jnp.int32, (TILE, size), 1)
    sub = lax.broadcasted_iota(jnp.int32, (TILE, size), 0)
    keep = lax.broadcasted_iota(jnp.int32, (size - TILE, size), 1) >= TILE

    def spread(column):
        return jnp.broadcast_to(column, (TILE, size))

    def trip(_, carried):
        real, imag = carried
        top_r, top_i = real[:TILE], imag[:TILE]
        columns = [
            (spread(top_r[:, j : j + 1]), spread(top_i[:, j : j + 1])) for j in range(TILE)
        ]
        for k in range(TILE):
            col_r, col_i = columns[k]
            pivot_r, pivot_i = col_r[k : k + 1], col_i[k : k + 1]
            scale = reciprocal(pivot_r * pivot_r + pivot_i * pivot_i)
            q_r, q_i = pivot_r * scale, -pivot_i * scale
            at = sub == k
            col_r, col_i = jnp.where(at, -1.0, col_r), jnp.where(at, 0.0, col_i)
            for j in range(k + 1, TILE):
                old_r, old_i = columns[j]
                t_r, t_i = times(old_r[k : k + 1], old_i[k : k + 1], q_r, q_i)
                u_r, u_i = times(col_r, col_i, t_r, t_i)
                columns[j] = (jnp.where(at, 0.0, old_r) - u_r, jnp.where(at, 0.0, old_i) - u_i)
            row_r, row_i = times(top_r[k : k + 1], top_i[k : k + 1], q_r, q_i)
            here = lane[:1] == k
            row_r, row_i = jnp.where(here, q_r, row_r), jnp.where(here, q_i, row_i)
            u_r, u_i = times(col_r, col_i, row_r, row_i)
            gone = at | (lane == k)
            top_r = jnp.where(gone, 0.0, top_r) - u_r
            top_i = jnp.where(gone, 0.0, top_i) - u_i
        old_r, old_i = real[TILE:], imag[TILE:]
        new_r, new_i = jnp.where(keep, old_r, 0.0), jnp.where(keep, old_i, 0.0)
        for k in range(TILE):
            u_r, u_i = times(
                old_r[:, k : k + 1], old_i[:, k : k + 1], top_r[k : k + 1], top_i[k : k + 1]
            )
            new_r, new_i = new_r - u_r, new_i - u_i
        real = jnp.concatenate([new_r, top_r], axis=0)
        imag = jnp.concatenate([new_i, top_i], axis=0)
        return pltpu.roll(real, size - TILE, 1), pltpu.roll(imag, size - TILE, 1)

    estimate = lax.fori_loop(0, size // TILE, trip, block)
    residue = product(block, estimate)
    one = jnp.where(eye(size), 1.0, 0.0)
    fix = product(estimate, (one - residue[0], -residue[1]), lax.Precision.DEFAULT)
    return (estimate[0] + fix[0], estimate[1] + fix[1])


def wire(count, energy_ref, broad_ref, onsite_ref, mix_ref, hop_ref, hopmix_ref, real_ref, imag_ref,
         crit_out, crit_in, rest_out, rest_in, own_ref, crit_sent, crit_got, rest_sent, rest_got):
    levels = count.bit_length() - 1
    size = mix_ref.shape[1]
    me = lax.axis_index("slab")

    def bit(stride):
        return (me // stride) % 2

    def partner(stride):
        return me + stride - 2 * stride * bit(stride)

    def copies(level, stride):
        target = {"slab": partner(stride)}
        return tuple(
            pltpu.make_async_remote_copy(
                src_ref=out.at[level], dst_ref=into.at[level], send_sem=sent.at[level],
                recv_sem=got.at[level], device_id=target,
                device_id_type=pl.DeviceIdType.MESH,
            )
            for out, into, sent, got in (
                (crit_out, crit_in, crit_sent, crit_got),
                (rest_out, rest_in, rest_sent, rest_got),
            )
        )

    barrier = pltpu.get_barrier_semaphore()
    for level in range(levels):
        pl.semaphore_signal(
            barrier, inc=1, device_id={"slab": partner(1 << level)},
            device_id_type=pl.DeviceIdType.MESH,
        )

    unit = eye(size)
    diagonal_i = jnp.where(unit, broad_ref[0], 0.0)

    def onsite(k):
        mixing = mix_ref[k]
        diagonal = jnp.where(unit, energy_ref[0] - onsite_ref[k : k + 1, :], 0.0)
        return diagonal - 0.5 * (mixing + mixing.T)

    def coupling(k):
        return jnp.where(unit, hop_ref[k : k + 1, :], 0.0) + hopmix_ref[k]

    middle = inverse((onsite(1), diagonal_i))
    lower = coupling(0)
    upper = jnp.where(me == count - 1, 0.0, coupling(1))
    weighted = dot(
        jnp.concatenate([middle[0], middle[1]], axis=0),
        jnp.concatenate([lower.T, upper], axis=1),
    )
    to_low = (weighted[:size, :size], weighted[size:, :size])
    to_high = (weighted[:size, size:], weighted[size:, size:])
    outs = dot(
        jnp.concatenate([lower, upper.T], axis=0),
        jnp.concatenate([to_low[0], to_low[1], to_high[0], to_high[1]], axis=1),
    )
    alpha = (onsite(0) - outs[:size, :size], diagonal_i - outs[:size, size : 2 * size])
    link = (outs[:size, 2 * size : 3 * size], outs[:size, 3 * size :])
    beta = (outs[size:, 2 * size : 3 * size], outs[size:, 3 * size :])
    high = bit(1) > 0
    write(crit_out, chosen(high, alpha, beta), 0, 0)
    write(rest_out, link, 0, 0)
    write(rest_out, chosen(high, beta, alpha), 0, 2)
    zero = jnp.zeros((size, size), jnp.float32)
    one = jnp.where(unit, 1.0, 0.0)
    write(own_ref, (zero, zero), 0, 0)
    write(own_ref, (one, zero), 0, 2)
    write(own_ref, (zero, zero), 0, 4)
    write(own_ref, middle, 1, 0)
    write(own_ref, to_low, 1, 2)
    write(own_ref, to_high, 1, 4)
    pl.semaphore_wait(barrier, levels)
    for copy in copies(0, 1):
        copy.start()

    def eliminated(level, high):
        sign = jnp.where(high, 1.0, -1.0)
        mine, other = read(crit_out, level, 0), read(crit_in, level, 0)
        return inverse((sign * (mine[0] - other[0]), sign * (mine[1] - other[1])))

    def links(level, high):
        mine, other = read(rest_out, level, 0), read(rest_in, level, 0)
        return chosen(high, other, mine), chosen(high, mine, other)

    def ends(level, high):
        mine, other = read(rest_out, level, 2), read(rest_in, level, 2)
        return chosen(high, other, mine), chosen(high, mine, other)

    def step(level, stride):
        high = bit(stride) > 0
        crit, rest = copies(level, stride)
        crit.wait_recv()
        y = eliminated(level, high)
        rest.wait_recv()
        low_link, high_link = links(level, high)
        alpha, beta = ends(level, high)
        legs = cols(flipped(low_link), high_link)
        weighted = product(rows(low_link, flipped(high_link)), y)
        outs = product(weighted, legs)
        alpha = tuple(a - o[:size, :size] for a, o in zip(alpha, outs))
        link = tuple(o[:size, size:] for o in outs)
        beta = tuple(b + o[size:, size:] for b, o in zip(beta, outs))
        following = bit(2 * stride) > 0
        write(crit_out, chosen(following, alpha, beta), level + 1, 0)
        write(rest_out, link, level + 1, 0)
        write(rest_out, chosen(following, beta, alpha), level + 1, 2)
        for copy in copies(level + 1, 2 * stride):
            copy.start()
        states = [[read(own_ref, k, 2 * piece) for piece in range(3)] for k in range(2)]
        used = [chosen(high, state[1], state[2]) for state in states]
        weighted = product(rows(*used), y)
        moved = product(weighted, legs)
        for k, state in enumerate(states):
            part = slice(k * size, (k + 1) * size)
            own = product((weighted[0][part], weighted[1][part]), flipped(used[k]))
            write(own_ref, tuple(s + o for s, o in zip(state[0], own)), k, 0)
            down = tuple(
                jnp.where(high, 0.0, s) + m[part, :size] for s, m in zip(state[1], moved)
            )
            up = tuple(
                jnp.where(high, s, 0.0) + m[part, size:] for s, m in zip(state[2], moved)
            )
            write(own_ref, down, k, 2)
            write(own_ref, up, k, 4)
        return 2 * stride

    stride = lax.fori_loop(0, levels - 1, step, jnp.int32(1))
    last = levels - 1
    high = bit(stride) > 0
    crit, rest = copies(last, stride)
    crit.wait_recv()
    y = eliminated(last, high)
    rest.wait_recv()
    low_link, _ = links(last, high)
    alpha, _ = ends(last, high)
    across = flipped(low_link)
    outs = product(product(low_link, y), across)
    top = inverse((alpha[0] - outs[0], alpha[1] - outs[1]))
    states = [[read(own_ref, k, 2 * piece) for piece in range(3)] for k in range(2)]
    used = [chosen(high, state[1], state[2]) for state in states]
    weighted = product(rows(*used), y)
    moved = product(weighted, across)
    legs = [
        tuple(
            jnp.where(high, 0.0, s) + m[k * size : (k + 1) * size] for s, m in zip(states[k][1], moved)
        )
        for k in range(2)
    ]
    carried = product(rows(*legs), top)
    for k in range(2):
        part = slice(k * size, (k + 1) * size)
        own = product(
            cols((weighted[0][part], weighted[1][part]), (carried[0][part], carried[1][part])),
            rows(flipped(used[k]), flipped(legs[k])),
        )
        real_ref[k] = states[k][0][0] + own[0]
        imag_ref[k] = states[k][0][1] + own[1]

    def drain(level, stride):
        for copy in copies(level, stride):
            copy.wait_send()
        return 2 * stride

    lax.fori_loop(0, levels, drain, jnp.int32(1))


def shards(onsite_energy, onsite_mixing, hop_strength, hop_mixing, energy, broadening):
    size = onsite_mixing.shape[1]
    count = lax.axis_size("slab")
    levels = count.bit_length() - 1
    vmem = pl.BlockSpec(memory_space=pltpu.VMEM)
    smem = pl.BlockSpec(memory_space=pltpu.SMEM)
    out = jax.ShapeDtypeStruct(onsite_mixing.shape, jnp.float32)
    crit = pltpu.VMEM((levels, 2, size, size), jnp.float32)
    rest = pltpu.VMEM((levels, 4, size, size), jnp.float32)
    return pl.pallas_call(
        functools.partial(wire, count),
        out_shape=[out, out],
        in_specs=[smem] * 2 + [vmem] * 4,
        out_specs=[vmem, vmem],
        scratch_shapes=[crit, crit, rest, rest, pltpu.VMEM((2, 6, size, size), jnp.float32)]
        + [pltpu.SemaphoreType.DMA((levels,))] * 4,
        compiler_params=pltpu.CompilerParams(collective_id=0, has_side_effects=True),
        name="wire",
    )(energy, broadening, onsite_energy, onsite_mixing, hop_strength, hop_mixing)


def solution(mesh):
    return jax.shard_map(
        shards,
        mesh=mesh,
        in_specs=(
            P("slab", None),
            P("slab", None, None),
            P("slab", None),
            P("slab", None, None),
            P("energy"),
            P("energy"),
        ),
        out_specs=(P(("energy", "slab"), None, None), P(("energy", "slab"), None, None)),
        check_vma=False,
    )
```

time: 159 us -> 95.1 us (0.60)
  Pallas kernels: 128 us -> 90.7 us
  starting transfers between devices: 12.3 us -> 0 us
  waiting for transfers between devices: 6.49 us -> 0 us
  other arithmetic: 4.02 us -> 0 us
  local copies, waits for them, and re-layouts: 5.57 us -> 2.26 us
    pallas_call x14 -> x1, Pallas kernels: 128 us -> 90.7 us  [shards(): pl.pallas_call(functools.partial(wire, count), out_shape=[out, out], in_s...]
    ppermute x8 -> x0, starting transfers between devices: 12.3 us -> none  [the longest x4 10.2 us: shards(): crit_other = lax.ppermute(crit, 'slab', pairs)]
    ppermute x8 -> x0, waiting for transfers between devices: 6.49 us -> none  [the longest x4 6.48 us: shards(): crit_other = lax.ppermute(crit, 'slab', pairs)]
    another operation x6 -> x0, other arithmetic: 4.01 us -> none  [the longest x4 2.52 us: shards(): flags = jnp.stack([bit(level), bit(level + 1)])]
    unnamed x20 -> x4, local copies, waits for them, and re-layouts: 5.49 us -> 2.26 us
  transfers between devices with their start and end apart: 8 -> 0, of which waited for: 3 -> 0; matrix products, arithmetic and copies ran while one was open for 2% -> 0% of each run, Pallas kernels for 49% -> 0%
where the time goes in v2:
time: 95.1 us; the launch traced here: 94.9 us
  Pallas kernels  90.7 us (95%)
  local copies, waits for them, and re-layouts  2.26 us (2%)
  between operations  1.94 us (2%)
    pallas_call x1, Pallas kernels, shards(): pl.pallas_call(functools.partial(wire, count), out_shape=[out, out], in_s...  90.7 us
    unnamed x4, local copies, waits for them, and re-layouts  2.26 us

profile of v2, /device:TPU:0, one launch (start us, length us, event | category | flops | bytes accessed | tf_op | source)
XLA Modules:
  0.0 94.9 jit_solution(12596507618266372982)
XLA Ops:
  1.9 90.7 %wire.1 = (f32[2,128,128]{2,1,0:T(8,128)}, f32[2,128,128]{2,1,0:T(8,128)}) custom-call(f32[1]{0:T(128)S(6)} %copy.10.energy_ref, f32[1]{0:T(128)S(6)} %copy.11.broad_ref, f32[2,128]{1,0:T(2,128)} %onsite_ref.1, f32[2,128,128]{2,1,0:T(8,128)} %mix_ref.1, f32[2,128]{1,0:T(2,128)} %hop_ref.1, f32[2,128,128]{2,1,0:T(8,128)} %hopmix_ref.1), custom_call_target="tpu_custom_call" | custom-call | tf_op jit(solution)/shard_map/wire/pallas_call | solution.py:300
  92.7 0.0 copy-start
  92.7 1.6 %copy.12 = f32[2,128,128]{2,1,0:T(8,128)} copy(f32[2,128,128]{2,1,0:T(8,128)} %get-tuple-element.4) | data formatting | bytes 262144
  94.3 0.0 copy-done
  94.3 0.7 copy.13
Async XLA Ops:
  92.7 1.6 %copy-start = (f32[2,128,128]{2,1,0:T(8,128)S(1)}, f32[2,128,128]{2,1,0:T(8,128)}, u32[]{:S(2)}) copy-start(f32[2,128,128]{2,1,0:T(8,128)} %get-tuple-element.5) | copy-start | bytes 393220
